TPU v7x, 32 devices: a whole 2x2x4 slice. The times are simulated.
32 devices in a mesh: out: 8 (over z, x), inp: 4 (over y, core).
Axes of the slice: x: 2, y: 2, z: 4, core: 2. Of those that a mesh axis runs over, the one named last changes fastest.
Arguments:
- tensor: bfloat16 [1024, 1024, 1024], P('out', 'inp'), may hold values from -0.005859375 to 0.005859375
- state: bfloat16 [768, 1024], P('out'), may hold values from -6 to 6
Outputs:
- collision: bfloat16 [768, 1024], P('inp', 'out')
All inputs are finite; a program needn't handle non-finite values.
Results may differ from a plain program's by a relative error of at most 0.001.
Values may be sent and summed in bfloat16 or wider, within the bound.
A program may use at most 128 MiB of HBM per device.

v0:
```python
import jax
import jax.numpy as jnp
from jax import lax
from jax.sharding import PartitionSpec as P


def local(tensor, state):
    rows_out = tensor.shape[0]
    rows_inp = tensor.shape[1]
    width = tensor.shape[2]
    flat = tensor.reshape(rows_out * rows_inp, width)
    first_col = lax.axis_index("inp") * rows_inp
    piece = lax.all_gather(state, "out", axis=0, tiled=True)
    inner = lax.dot_general(
        piece, flat, (((1,), (1,)), ((), ())), preferred_element_type=jnp.float32
    )
    inner = inner.reshape(piece.shape[0], rows_out, rows_inp)
    chosen = lax.dynamic_slice_in_dim(piece, first_col, rows_inp, 1).astype(jnp.float32)
    partial_sum = jnp.sum(inner * chosen[:, None, :], axis=2)
    owned = lax.psum_scatter(partial_sum, "inp", scatter_dimension=0, tiled=True)
    return owned.astype(jnp.bfloat16)


def solution(mesh):
    placed = (P("out", "inp", None), P("out", None))
    return jax.shard_map(
        local, mesh=mesh, in_specs=placed, out_specs=P("inp", "out"), check_vma=False
    )
```

profile of v0, /device:TPU:0, one launch (start us, length us, event | category | flops | bytes accessed | tf_op | source)
XLA Modules:
  0.0 146.9 jit_solution(9233174708893492193)
XLA Ops:
  6.5 0.0 all-gather.2.cloned.1.call-start
  6.5 0.7 all-gather.2.cloned.1.call-update
  7.3 0.0 reduce-scatter.4.cloned.1.call-start
  7.3 49.1 %all-gather.2.cloned.1.call-done = bf16[768,1024]{1,0:T(8,128)(2,1)} async-done(((bf16[96,1024]{1,0:T(8,128)(2,1)}), bf16[768,1024]{1,0:T(8,128)(2,1)}) %all-gather.2.cloned.1.call-update) | async-done | bytes 1572880 | tf_op jit(solution)/shard_map/all_gather | solution.py:13
  56.4 1.0 dynamic-slice_convert_fusion
  57.5 0.3 copy.8
  57.8 60.4 %multiply_reduce_fusion = f32[768,128]{0,1:T(8,128)S(1)} fusion(f32[768,256]{0,1:T(8,128)S(1)} %copy.8, bf16[128,256,1024]{2,1,0:T(8,128)(2,1)} %param.2, bf16[768,1024]{1,0:T(8,128)(2,1)} %all-gather.2.cloned.1.call-done), kind=kOutput, calls=%fused_computation | convolution fusion | flops 51589840896 | bytes 69861376 | tf_op jit(solution)/shard_map/dot_general | solution.py:14
  118.2 0.9 copy.10
  119.1 0.0 reduce-scatter.4.cloned.1.call-update
  119.1 19.3 %reduce-scatter.4.cloned.1.call-done = f32[192,128]{1,0:T(8,128)} async-done(((f32[768,128]{1,0:T(8,128)}), f32[192,128]{1,0:T(8,128)}) %reduce-scatter.4.cloned.1.call-update) | async-done | bytes 98320 | tf_op jit(solution)/shard_map/reduce_scatter | solution.py:20
  138.5 1.5 %convert_element_type.7 = bf16[192,128]{1,0:T(8,128)(2,1)} convert(f32[192,128]{1,0:T(8,128)} %reduce-scatter.4.cloned.1.call-done) | non-fusion elementwise | flops 24576 | bytes 147456 | tf_op jit(solution)/shard_map/convert_element_type | solution.py:21
Async XLA Ops:
  6.5 49.9 %all-gather.2.cloned.1.call-start = ((), (), s32[]{:S(2)}) async-start(), calls=%async_computation.1 | async-start | bytes 1769472 | tf_op jit(solution)/shard_map/all_gather | solution.py:13
  7.3 131.2 %reduce-scatter.4.cloned.1.call-start = ((), (), s32[]{:S(2)}) async-start(), calls=%async_computation.2 | async-start | bytes 491520 | tf_op jit(solution)/shard_map/reduce_scatter | solution.py:20
Sparse Core Ops, SparseCore 0:
  9.5 46.8 all-gather.1
  119.3 19.1 reduce-scatter.3
where the time goes:
time: 147 us
  waiting for transfers between devices  69.2 us (47%)
  matrix products  60.4 us (41%)
  between operations  13.4 us (9%)
  other arithmetic  2.56 us (2%)
    dot_general x1, matrix products, local(): lax.dot_general(piece, flat, (((1,), (1,)), ((), ())), preferred_element_...  60.4 us
    all_gather x1, waiting for transfers between devices, local(): piece = lax.all_gather(state, 'out', axis=0, tiled=True)  49.1 us
    reduce_scatter x1, waiting for transfers between devices, local(): lax.psum_scatter(partial_sum, 'inp', scatter_dimension=0, tiled=True)  19.3 us
  transfers between devices with their start and end apart: 2, of which 2 were waited for; matrix products, arithmetic and copies ran while one was open for 0% of the time, Pallas kernels for 0%

commit v1 on v0

v1 whole, which is shorter than its diff:
```python
import functools

import jax
import jax.numpy as jnp
from jax import lax
from jax.experimental import pallas as pl
from jax.experimental.pallas import tpu as pltpu
from jax.sharding import PartitionSpec as P

MESH = pl.DeviceIdType.MESH
GROUP = 8
SLOTS = 4


def kernel(nx, n_out, n_inp, tensor, state, out, gathered, turned, chosen, slab, parts, landed,
           own_sems, z_sems, x_sems, core_sems, t_sems, s_sems, r_sems):
    rows_out, rows_inp, width = tensor.shape
    cells_own = state.shape[0]
    cells = n_out * cells_own
    nz = n_out // nx
    per_owner = n_out // n_inp
    blocks = rows_out // GROUP
    slots = slab.shape[0]
    lanes = 256 if cells % 256 == 0 else cells
    halves = 2
    half_width = width // halves

    me_o = lax.axis_index("out")
    me_p = lax.axis_index("inp")
    z, x = me_o // nx, me_o % nx
    half = me_p % halves
    partner = me_p + 1 - 2 * half
    cols = pl.ds(pl.multiple_of(half * half_width, 128), half_width)
    other_cols = pl.ds(pl.multiple_of((1 - half) * half_width, 128), half_width)

    def fetch(b, slot):
        return pltpu.make_async_copy(
            tensor.at[pl.ds(b * GROUP, GROUP)], slab.at[slot], t_sems.at[slot])

    for b in range(min(slots, blocks)):
        fetch(b, b).start()

    def out_of(zz, xx):
        return lax.rem(zz + nz, nz) * nx + lax.rem(xx + nx, nx)

    barrier = pltpu.get_barrier_semaphore()
    near = [(out_of(z + d, x), me_p) for d in range(1, nz)]
    near += [(out_of(z, x + e), me_p) for e in range(1, nx)]
    near += [(me_o, lax.rem(me_p + q, n_inp)) for q in range(1, n_inp)]
    for device in near:
        pl.semaphore_signal(barrier, inc=1, device_id=device, device_id_type=MESH)
    pl.semaphore_wait(barrier, len(near))

    def remote(src, dst, send, recv, device):
        return pltpu.make_async_remote_copy(
            src_ref=src, dst_ref=dst, send_sem=send, recv_sem=recv,
            device_id=device, device_id_type=MESH)

    def z_copy(d):
        return remote(state.at[:, cols], gathered.at[me_o, :, cols], z_sems.at[0, d],
                      z_sems.at[1, d], (out_of(z + d, x), me_p))

    def x_copy(e, d):
        shard = out_of(z - d, x)
        src = state.at[:, cols] if d == 0 else gathered.at[shard, :, cols]
        return remote(src, gathered.at[shard, :, cols], x_sems.at[0, e, d], x_sems.at[1, e, d],
                      (out_of(z, x + e), me_p))

    def core_copy(e, d):
        shard = out_of(z - d, x - e)
        block = gathered.at[shard, :, cols]
        return remote(block, block, core_sems.at[0, e, d], core_sems.at[1, e, d], (me_o, partner))

    started = []

    def start(copy):
        copy.start()
        started.append(copy)

    for e in range(1, nx):
        start(x_copy(e, 0))
    for d in range(1, nz):
        start(z_copy(d))
    gathered[me_o] = state[...]
    for e in range(1, nx):
        x_copy(e, 0).wait_recv()
        start(core_copy(e, 0))
    for d in range(1, nz):
        z_copy(d).wait_recv()
        for e in range(1, nx):
            start(x_copy(e, d))
        start(core_copy(0, d))
    for d in range(1, nz):
        for e in range(1, nx):
            x_copy(e, d).wait_recv()
            start(core_copy(e, d))
    for d in range(nz):
        for e in range(nx):
            if (e, d) != (0, 0):
                core_copy(e, d).wait_recv()

    for j in range(0, width, 128):
        piece = gathered[:, :, j:j + 128].reshape(cells, 128)
        turned[j:j + 128, :] = piece.T
    first = pl.multiple_of(me_p * rows_inp, rows_inp)
    chosen[...] = turned[pl.ds(first, rows_inp), :].astype(jnp.float32)

    def send_part(b, q):
        owner = lax.rem(me_p + q, n_inp)
        rows = pl.ds(pl.multiple_of(b * GROUP, GROUP), GROUP)
        return remote(parts.at[pl.ds(owner * per_owner, per_owner), rows],
                      landed.at[q - 1, :, rows],
                      s_sems.at[q - 1], r_sems.at[q - 1], (me_o, owner))

    def compute(b, carry):
        slot = lax.rem(b, slots)
        fetch(b, slot).wait()
        pieces = []
        for n in range(0, cells, lanes):
            sums = []
            for k in range(GROUP):
                inner = jnp.dot(slab[slot, k], turned[:, n:n + lanes],
                                preferred_element_type=jnp.float32)
                sums.append(jnp.sum(inner * chosen[:, n:n + lanes], axis=0, keepdims=True))
            pieces.append(jnp.concatenate(sums, axis=0))
        total = jnp.concatenate(pieces, axis=1)
        rows = pl.ds(pl.multiple_of(b * GROUP, GROUP), GROUP)
        for s in range(n_out):
            parts[s, rows, 0:cells_own] = total[:, s * cells_own:(s + 1) * cells_own]

        @pl.when(b + slots < blocks)
        def _():
            fetch(b + slots, slot).start()

        for q in range(1, n_inp):
            send_part(b, q).start()
        return carry

    lax.fori_loop(0, blocks, compute, 0)

    for copy in started:
        copy.wait_send()
    everything = [remote(parts.at[pl.ds(0, per_owner)], landed.at[q - 1], s_sems.at[q - 1],
                         r_sems.at[q - 1], (me_o, lax.rem(me_p + q, n_inp))) for q in range(1, n_inp)]
    for copy in everything:
        copy.wait_recv()
    for s in range(per_owner):
        total = parts[me_p * per_owner + s]
        for q in range(1, n_inp):
            total = total + landed[q - 1, s]
        out[s * cells_own:(s + 1) * cells_own, :] = total.T[0:cells_own, :].astype(out.dtype)
    for copy in everything:
        copy.wait_send()


def solution(mesh):
    n_out, n_inp = mesh.shape["out"], mesh.shape["inp"]
    nx = len({device.coords[0] for device in mesh.devices[:, 0]})

    def local(tensor, state):
        rows_out, rows_inp, width = tensor.shape
        cells_own = state.shape[0]
        cells = n_out * cells_own
        per_owner = n_out // n_inp
        padded = -(-cells_own // 128) * 128
        nz = n_out // nx
        return pl.pallas_call(
            functools.partial(kernel, nx, n_out, n_inp),
            out_shape=jax.ShapeDtypeStruct((cells // n_inp, rows_out), jnp.bfloat16),
            in_specs=[pl.BlockSpec(memory_space=pl.ANY), pl.BlockSpec(memory_space=pltpu.VMEM)],
            out_specs=pl.BlockSpec(memory_space=pltpu.VMEM),
            scratch_shapes=[
                pltpu.VMEM((n_out, cells_own, width), jnp.bfloat16),
                pltpu.VMEM((width, cells), jnp.bfloat16),
                pltpu.VMEM((rows_inp, cells), jnp.float32),
                pltpu.VMEM((SLOTS, GROUP, rows_inp, width), jnp.bfloat16),
                pltpu.VMEM((n_out, rows_out, padded), jnp.float32),
                pltpu.VMEM((n_inp - 1, per_owner, rows_out, padded), jnp.float32),
                pltpu.SemaphoreType.DMA((2,)),
                pltpu.SemaphoreType.DMA((2, nz)),
                pltpu.SemaphoreType.DMA((2, nx, nz)),
                pltpu.SemaphoreType.DMA((2, nx, nz)),
                pltpu.SemaphoreType.DMA((SLOTS,)),
                pltpu.SemaphoreType.DMA((n_inp - 1,)),
                pltpu.SemaphoreType.DMA((n_inp - 1,)),
            ],
            compiler_params=pltpu.CompilerParams(
                collective_id=0, has_side_effects=True, vmem_limit_bytes=60 * 2**20),
            name="collide",
        )(tensor, state)

    return jax.shard_map(
        local, mesh=mesh, in_specs=(P("out", "inp", None), P("out", None)),
        out_specs=P("inp", "out"), check_vma=False)
```

time: 147 us -> 82.7 us (0.56)
  Pallas kernels: 0 us -> 81.1 us
  waiting for transfers between devices: 69.2 us -> 0 us
  matrix products: 60.4 us -> 0 us
  between operations: 13.4 us -> 0.01 us
  other arithmetic: 2.56 us -> 0 us
    pallas_call x0 -> x1, Pallas kernels: none -> 81.1 us  [local(): pl.pallas_call(functools.partial(kernel, nx, n_out, n_inp), out_shape=jax...]
    dot_general x1 -> x0, matrix products: 60.4 us -> none  [local(): lax.dot_general(piece, flat, (((1,), (1,)), ((), ())), preferred_element_...]
    all_gather x1 -> x0, waiting for transfers between devices: 49.1 us -> none  [local(): piece = lax.all_gather(state, 'out', axis=0, tiled=True)]
    reduce_scatter x1 -> x0, waiting for transfers between devices: 19.3 us -> none  [local(): lax.psum_scatter(partial_sum, 'inp', scatter_dimension=0, tiled=True)]
    convert_element_type x2 -> x0, other arithmetic: 2.56 us -> none  [the longest x1 1.52 us: local(): return owned.astype(jnp.bfloat16)]
  transfers between devices with their start and end apart: 2 -> 0, of which waited for: 2 -> 0; matrix products, arithmetic and copies ran while one was open for 0% -> 0% of each run, Pallas kernels for 0% -> 0%
where the time goes in v1:
time: 82.7 us; the launch traced here: 82.5 us
  Pallas kernels  81.1 us (98%)
  local copies, waits for them, and re-layouts  1.42 us (2%)
    pallas_call x1, Pallas kernels, local(): pl.pallas_call(functools.partial(kernel, nx, n_out, n_inp), out_shape=jax...  81.1 us

profile of v1, /device:TPU:0, one launch (start us, length us, event | category | flops | bytes accessed | tf_op | source)
XLA Modules:
  0.0 82.5 jit_solution(6709789012669310207)
XLA Ops:
  0.0 81.1 %collide.1 = bf16[192,128]{1,0:T(8,128)(2,1)} custom-call(bf16[128,256,1024]{2,1,0:T(8,128)(2,1)} %tensor.1, bf16[96,1024]{1,0:T(8,128)(2,1)} %state.1), custom_call_target="tpu_custom_call" | custom-call | tf_op jit(solution)/shard_map/collide/pallas_call | solution.py:167
  81.1 1.4 %copy.4 = bf16[192,128]{1,0:T(8,128)(2,1)} copy(bf16[192,128]{1,0:T(8,128)(2,1)} %collide.1) | data formatting | bytes 98304

commit v2 on v1

v2 whole, which is shorter than its diff:
```python
import functools

import jax
import jax.numpy as jnp
from jax import lax
from jax.experimental import pallas as pl
from jax.experimental.pallas import tpu as pltpu
from jax.sharding import PartitionSpec as P

MESH = pl.DeviceIdType.MESH
GROUP = 16
SLOTS = 5


def flip(value, bits):
    for bit in (1 << n for n in range(bits.bit_length())):
        if bits & bit:
            value = value + bit * (1 - 2 * ((value // bit) % 2))
    return value


def kernel(nx, n_out, n_inp, tensor, state, out, gathered, turned, chosen, slab, parts, landed,
           z_sems, x_sems, core_sems, t_sems, s_sems, r_sems):
    rows_out, rows_inp, width = tensor.shape
    cells_own = state.shape[0]
    cells = n_out * cells_own
    nz = n_out // nx
    per_owner = n_out // n_inp
    group = slab.shape[1]
    blocks = rows_out // group
    slots = slab.shape[0]
    lanes = 256 if cells % 256 == 0 else cells
    halves = 2
    half_width = width // halves
    early = -(-lanes // cells_own)

    me_o = lax.axis_index("out")
    me_p = lax.axis_index("inp")
    z, x = me_o // nx, me_o % nx
    half = me_p % halves
    partner = me_p + 1 - 2 * half
    cols = pl.ds(pl.multiple_of(half * half_width, 128), half_width)

    def fetch(b, slot):
        return pltpu.make_async_copy(
            tensor.at[pl.ds(b * group, group)], slab.at[slot], t_sems.at[slot])

    for b in range(slots):
        fetch(b, b).start()

    def out_of(d, e):
        return flip(z, d) * nx + flip(x, e)

    barrier = pltpu.get_barrier_semaphore()
    near = [(out_of(d, 0), me_p) for d in range(1, nz)]
    near += [(out_of(0, e), me_p) for e in range(1, nx)]
    near += [(me_o, lax.rem(me_p + q, n_inp)) for q in range(1, n_inp)]
    for device in near:
        pl.semaphore_signal(barrier, inc=1, device_id=device, device_id_type=MESH)
    pl.semaphore_wait(barrier, len(near))

    def remote(src, dst, send, recv, device):
        return pltpu.make_async_remote_copy(
            src_ref=src, dst_ref=dst, send_sem=send, recv_sem=recv,
            device_id=device, device_id_type=MESH)

    def shard(d, e):
        return gathered.at[pl.ds((d * nx + e) * cells_own, cells_own), cols]

    def z_copy(d):
        return remote(state.at[:, cols], shard(d, 0), z_sems.at[0, d], z_sems.at[1, d],
                      (out_of(d, 0), me_p))

    def x_copy(e, d):
        return remote(state.at[:, cols] if d == 0 else shard(d, 0), shard(d, e),
                      x_sems.at[0, e, d], x_sems.at[1, e, d], (out_of(0, e), me_p))

    def core_copy(e, d):
        return remote(shard(d, e), shard(d, e), core_sems.at[0, e, d], core_sems.at[1, e, d],
                      (me_o, partner))

    def relay_x(d):
        for e in range(1, nx):
            x_copy(e, d).wait_recv()
            core_copy(e, d).start()

    def relay_z(d):
        z_copy(d).wait_recv()
        for e in range(1, nx):
            x_copy(e, d).start()
        core_copy(0, d).start()

    for e in range(1, nx):
        x_copy(e, 0).start()
    for d in range(1, nz):
        z_copy(d).start()
    gathered[0:cells_own, :] = state[...]
    relay_x(0)
    relay_z(1)
    order = [(d, e) for d in range(nz) for e in range(nx)]
    for d, e in order[1:early]:
        core_copy(e, d).wait_recv()

    first = pl.multiple_of(me_p * rows_inp, rows_inp)

    def turn(start, stop):
        for j in range(0, width, 128):
            turned[j:j + 128, start:stop] = gathered[start:stop, j:j + 128].T
        chosen[:, start:stop] = turned[pl.ds(first, rows_inp), start:stop].astype(jnp.float32)

    def send_part(b, q):
        owner = lax.rem(me_p + q, n_inp)
        rows = pl.ds(pl.multiple_of(b * group, group), group)
        return remote(parts.at[pl.ds(owner * per_owner, per_owner), rows],
                      landed.at[q - 1, :, rows],
                      s_sems.at[q - 1], r_sems.at[q - 1], (me_o, owner))

    def products(b, slot, start, stop):
        pieces = []
        for n in range(start, stop, lanes):
            sums = []
            for k in range(group):
                inner = jnp.dot(slab[slot, k], turned[:, n:n + lanes],
                                preferred_element_type=jnp.float32)
                sums.append(jnp.sum(inner * chosen[:, n:n + lanes], axis=0, keepdims=True))
            pieces.append(jnp.concatenate(sums, axis=0))
        total = jnp.concatenate(pieces, axis=1)
        rows = pl.ds(pl.multiple_of(b * group, group), group)
        for s, (d, e) in enumerate(order):
            low, high = max(start, s * cells_own), min(stop, (s + 1) * cells_own)
            if low < high:
                parts[out_of(d, e), rows, low - s * cells_own:high - s * cells_own] = (
                    total[:, low - start:high - start])

    def finish(b, slot):
        for q in range(1, n_inp):
            send_part(b, q).start()

        @pl.when(b + slots < blocks)
        def _():
            fetch(b + slots, slot).start()

    turn(0, lanes)

    def lead(b, carry):
        for d in range(2, nz + 1):
            @pl.when(b == min((d - 1) * slots // max(nz - 1, 1), slots - 1))
            def _():
                if d < nz:
                    relay_z(d)
                relay_x(d - 1)
        fetch(b, b).wait()
        products(b, b, 0, lanes)
        return carry

    lax.fori_loop(0, slots, lead, 0)
    for d, e in order[early:]:
        core_copy(e, d).wait_recv()
    if lanes < cells:
        turn(lanes, cells)

    def follow(b, carry):
        if lanes < cells:
            products(b, b, lanes, cells)
        finish(b, b)
        return carry

    lax.fori_loop(0, slots, follow, 0)

    def whole(b, carry):
        slot = lax.rem(b, slots)
        fetch(b, slot).wait()
        products(b, slot, 0, cells)
        finish(b, slot)
        return carry

    if slots < blocks:
        lax.fori_loop(slots, blocks, whole, 0)

    everything = [remote(parts.at[pl.ds(0, per_owner)], landed.at[q - 1], s_sems.at[q - 1],
                         r_sems.at[q - 1], (me_o, lax.rem(me_p + q, n_inp))) for q in range(1, n_inp)]
    for d in range(1, nz):
        z_copy(d).wait_send()
    for d, e in order:
        if e > 0:
            x_copy(e, d).wait_send()
        if (d, e) != (0, 0):
            core_copy(e, d).wait_send()
    for copy in everything:
        copy.wait_recv()
    for s in range(per_owner):
        total = parts[me_p * per_owner + s]
        for q in range(1, n_inp):
            total = total + landed[q - 1, s]
        out[s * cells_own:(s + 1) * cells_own, :] = total.T[0:cells_own, :].astype(out.dtype)
    for copy in everything:
        copy.wait_send()


def solution(mesh):
    n_out, n_inp = mesh.shape["out"], mesh.shape["inp"]
    nx = len({device.coords[0] for device in mesh.devices[:, 0]})

    def local(tensor, state):
        rows_out, rows_inp, width = tensor.shape
        cells_own = state.shape[0]
        cells = n_out * cells_own
        per_owner = n_out // n_inp
        padded = -(-cells_own // 128) * 128
        nz = n_out // nx
        group = min(GROUP, rows_out)
        slots = min(SLOTS, rows_out // group)
        return pl.pallas_call(
            functools.partial(kernel, nx, n_out, n_inp),
            out_shape=jax.ShapeDtypeStruct((cells // n_inp, rows_out), jnp.bfloat16),
            in_specs=[pl.BlockSpec(memory_space=pl.ANY), pl.BlockSpec(memory_space=pltpu.VMEM)],
            out_specs=pl.BlockSpec(memory_space=pltpu.VMEM),
            scratch_shapes=[
                pltpu.VMEM((cells, width), jnp.bfloat16),
                pltpu.VMEM((width, cells), jnp.bfloat16),
                pltpu.VMEM((rows_inp, cells), jnp.float32),
                pltpu.VMEM((slots, group, rows_inp, width), jnp.bfloat16),
                pltpu.VMEM((n_out, rows_out, padded), jnp.float32),
                pltpu.VMEM((n_inp - 1, per_owner, rows_out, padded), jnp.float32),
                pltpu.SemaphoreType.DMA((2, nz)),
                pltpu.SemaphoreType.DMA((2, nx, nz)),
                pltpu.SemaphoreType.DMA((2, nx, nz)),
                pltpu.SemaphoreType.DMA((slots,)),
                pltpu.SemaphoreType.DMA((n_inp - 1,)),
                pltpu.SemaphoreType.DMA((n_inp - 1,)),
            ],
            compiler_params=pltpu.CompilerParams(
                collective_id=0, has_side_effects=True, vmem_limit_bytes=60 * 2**20),
            name="collide",
        )(tensor, state)

    return jax.shard_map(
        local, mesh=mesh, in_specs=(P("out", "inp", None), P("out", None)),
        out_specs=P("inp", "out"), check_vma=False)
```

time: 82.7 us -> 76.4 us (0.924)
  Pallas kernels: 81.1 us -> 74.7 us
    pallas_call x1, Pallas kernels: 81.1 us -> 74.7 us  [local(): pl.pallas_call(functools.partial(kernel, nx, n_out, n_inp), out_shape=jax...]
where the time goes in v2:
time: 76.4 us; the launch traced here: 76.2 us
  Pallas kernels  74.7 us (98%)
  local copies, waits for them, and re-layouts  1.42 us (2%)
    pallas_call x1, Pallas kernels, local(): pl.pallas_call(functools.partial(kernel, nx, n_out, n_inp), out_shape=jax...  74.7 us

profile of v2, /device:TPU:0, one launch (start us, length us, event | category | flops | bytes accessed | tf_op | source)
XLA Modules:
  0.0 76.2 jit_solution(16358831089135851923)
XLA Ops:
  0.0 74.7 %collide.1 = bf16[192,128]{1,0:T(8,128)(2,1)} custom-call(bf16[128,256,1024]{2,1,0:T(8,128)(2,1)} %tensor.1, bf16[96,1024]{1,0:T(8,128)(2,1)} %state.1), custom_call_target="tpu_custom_call" | custom-call | tf_op jit(solution)/shard_map/collide/pallas_call | solution.py:213
  74.7 1.4 %copy.4 = bf16[192,128]{1,0:T(8,128)(2,1)} copy(bf16[192,128]{1,0:T(8,128)(2,1)} %collide.1) | data formatting | bytes 98304
